TPU v7x, 32 devices: a whole 2x2x4 slice. The times are simulated.
32 devices in a mesh: dp: 8 (over z, x), mp: 4 (over y, core).
Axes of the slice: x: 2, y: 2, z: 4, core: 2. Of those that a mesh axis runs over, the one named last changes fastest.
Arguments:
- tokens: bfloat16 [16384, 1024], P('dp'), may hold values from -6 to 6
- cotangent: bfloat16 [16384, 1024], P('dp'), may hold values from -15 to 15
- item_lengths: int32 [8, 8], P('dp'), may hold values from 1 to 1024, 2048 in all within a row
- w_qkv: bfloat16 [3, 1024, 1024], P(None, None, 'mp'), may hold values from -0.1875 to 0.1875
- b_qv: float32 [2, 1024], P(None, 'mp'), may hold values from -3 to 3
- w_out: bfloat16 [1024, 1024], P('mp'), may hold values from -0.75 to 0.75
- b_out: float32 [1024], replicated, may hold values from -1.75 to 1.75
- w_fc1: bfloat16 [1024, 4096], P(None, 'mp'), may hold values from -0.1875 to 0.1875
- b_fc1: float32 [4096], P('mp'), may hold values from -3 to 3
- w_fc2: bfloat16 [4096, 1024], P('mp'), may hold values from -0.09375 to 0.09375
- b_fc2: float32 [1024], replicated, may hold values from -1.75 to 1.75
- ln1_gain: float32 [1024], replicated, may hold values from 0.5 to 1.5
- ln1_bias: float32 [1024], replicated, may hold values from -1.75 to 1.75
- ln2_gain: float32 [1024], replicated, may hold values from 0.5 to 1.5
- ln2_bias: float32 [1024], replicated, may hold values from -1.75 to 1.75
Outputs:
- output: bfloat16 [16384, 1024], P('dp')
- grad_tokens: float32 [16384, 1024], P('dp')
- grad_w_qkv: float32 [3, 1024, 1024], P(None, 'dp', 'mp')
- grad_b_qv: float32 [2, 1024], P(None, 'mp')
- grad_w_out: float32 [1024, 1024], P('mp', 'dp')
- grad_b_out: float32 [1024], replicated
- grad_w_fc1: float32 [1024, 4096], P('dp', 'mp')
- grad_b_fc1: float32 [4096], P('mp')
- grad_w_fc2: float32 [4096, 1024], P('mp', 'dp')
- grad_b_fc2: float32 [1024], replicated
- grad_ln1_gain: float32 [1024], replicated
- grad_ln1_bias: float32 [1024], replicated
- grad_ln2_gain: float32 [1024], replicated
- grad_ln2_bias: float32 [1024], replicated
Inputs may be any that keep to these rules, and one draw needn't show every extreme that they name: `item_lengths`: each row sums to 2048, and each row's longest item has exactly 1024 patches.
All inputs are finite; a program needn't handle non-finite values.
Results may differ from a plain program's by a relative error of at most 0.019.
Values may be sent and summed in bfloat16 or wider, within the bound.
A program may use at most 192 MiB of HBM per device.

v0:
```python
import jax
import jax.numpy as jnp
from jax import lax
from jax.sharding import PartitionSpec as P

HEAD = 64
QBLOCK = 512


def normalize(values, gain, shift):
    center = jnp.mean(values, axis=-1, keepdims=True)
    centered = values - center
    spread = jnp.mean(centered * centered, axis=-1, keepdims=True)
    return centered * lax.rsqrt(spread + 1e-06) * gain + shift


def exact_gelu(values):
    return jax.nn.gelu(values, approximate=False)


def segment_ids(lengths_row, row_count):
    ends = jnp.cumsum(lengths_row)
    positions = jnp.arange(row_count, dtype=jnp.int32)
    return jnp.sum((positions[:, None] >= ends[None, :]).astype(jnp.int32), axis=1)


def per_device(
    tokens,
    cotangent,
    item_lengths,
    w_qkv,
    b_qv,
    w_out,
    b_out,
    w_fc1,
    b_fc1,
    w_fc2,
    b_fc2,
    ln1_gain,
    ln1_bias,
    ln2_gain,
    ln2_bias,
):
    row_count = tokens.shape[0]
    local_cols = w_qkv.shape[2]
    heads_here = local_cols // HEAD
    blocks = row_count // QBLOCK
    score_scale = HEAD ** (-0.5)
    segments = segment_ids(item_lengths[0], row_count)
    seg_blocks = segments.reshape(blocks, QBLOCK)
    inputs = tokens.astype(jnp.float32)
    norm_one, norm_one_back = jax.vjp(normalize, inputs, ln1_gain, ln1_bias)
    normed_one = norm_one.astype(jnp.bfloat16)
    queries = (jnp.dot(normed_one, w_qkv[0], preferred_element_type=jnp.float32) + b_qv[0]).astype(
        jnp.bfloat16
    )
    key_rows = jnp.dot(normed_one, w_qkv[1], preferred_element_type=jnp.float32).astype(
        jnp.bfloat16
    )
    value_rows = (
        jnp.dot(normed_one, w_qkv[2], preferred_element_type=jnp.float32) + b_qv[1]
    ).astype(jnp.bfloat16)
    key_heads = key_rows.reshape(row_count, heads_here, HEAD)
    value_heads = value_rows.reshape(row_count, heads_here, HEAD)
    query_blocks = queries.reshape(blocks, QBLOCK, heads_here, HEAD)

    def block_scores(query_block, seg_block):
        scores = (
            jnp.einsum("qhd,khd->hqk", query_block, key_heads, preferred_element_type=jnp.float32)
            * score_scale
        )
        same = seg_block[:, None] == segments[None, :]
        return jnp.where(same[None], scores, -1e30)

    def forward_block(pieces):
        query_block, seg_block = pieces
        scores = block_scores(query_block, seg_block)
        row_max = jnp.max(scores, axis=-1, keepdims=True)
        raised = jnp.exp(scores - row_max)
        row_sum = jnp.sum(raised, axis=-1, keepdims=True)
        probs = raised / row_sum
        block_out = jnp.einsum(
            "hqk,khd->qhd",
            probs.astype(jnp.bfloat16),
            value_heads,
            preferred_element_type=jnp.float32,
        )
        return (block_out.astype(jnp.bfloat16), (row_max + jnp.log(row_sum))[..., 0])

    out_blocks, log_norms = lax.map(forward_block, (query_blocks, seg_blocks))
    attended = out_blocks.reshape(row_count, local_cols)
    attention_sum = lax.psum(
        jnp.dot(attended, w_out, preferred_element_type=jnp.float32).astype(jnp.bfloat16), "mp"
    ).astype(jnp.float32)
    middle = inputs + attention_sum + b_out
    norm_two, norm_two_back = jax.vjp(normalize, middle, ln2_gain, ln2_bias)
    normed_two = norm_two.astype(jnp.bfloat16)
    hidden_pre = jnp.dot(normed_two, w_fc1, preferred_element_type=jnp.float32) + b_fc1
    activated_full, gelu_back = jax.vjp(exact_gelu, hidden_pre)
    activated = activated_full.astype(jnp.bfloat16)
    mlp_sum = lax.psum(
        jnp.dot(activated, w_fc2, preferred_element_type=jnp.float32).astype(jnp.bfloat16), "mp"
    ).astype(jnp.float32)
    output = (middle + mlp_sum + b_fc2).astype(jnp.bfloat16)
    upstream = cotangent.astype(jnp.float32)
    grad_b_fc2 = jnp.sum(upstream, axis=0)
    grad_w_fc2 = jnp.einsum("tf,td->fd", activated, cotangent, preferred_element_type=jnp.float32)
    d_act = jnp.einsum("td,fd->tf", cotangent, w_fc2, preferred_element_type=jnp.float32)
    d_pre = gelu_back(d_act)[0]
    grad_b_fc1 = jnp.sum(d_pre, axis=0)
    d_pre_low = d_pre.astype(jnp.bfloat16)
    grad_w_fc1 = jnp.einsum("td,tf->df", normed_two, d_pre_low, preferred_element_type=jnp.float32)
    d_normed_two = lax.psum(
        jnp.einsum("tf,df->td", d_pre_low, w_fc1, preferred_element_type=jnp.float32).astype(
            jnp.bfloat16
        ),
        "mp",
    ).astype(jnp.float32)
    d_middle_norm, grad_ln2_gain, grad_ln2_bias = norm_two_back(d_normed_two)
    d_middle = upstream + d_middle_norm
    grad_b_out = jnp.sum(d_middle, axis=0)
    d_middle_low = d_middle.astype(jnp.bfloat16)
    grad_w_out = jnp.einsum("tc,td->cd", attended, d_middle_low, preferred_element_type=jnp.float32)
    d_attended = jnp.einsum(
        "td,cd->tc", d_middle_low, w_out, preferred_element_type=jnp.float32
    ).astype(jnp.bfloat16)
    d_att_blocks = d_attended.reshape(blocks, QBLOCK, heads_here, HEAD)

    def backward_block(running, pieces):
        d_keys_acc, d_values_acc = running
        query_block, seg_block, d_out_block, log_norm = pieces
        scores = block_scores(query_block, seg_block)
        probs = jnp.exp(scores - log_norm[..., None])
        d_probs = jnp.einsum(
            "qhd,khd->hqk", d_out_block, value_heads, preferred_element_type=jnp.float32
        )
        d_scores = probs * (d_probs - jnp.sum(probs * d_probs, axis=-1, keepdims=True))
        d_scores_low = d_scores.astype(jnp.bfloat16)
        d_query_block = (
            jnp.einsum("hqk,khd->qhd", d_scores_low, key_heads, preferred_element_type=jnp.float32)
            * score_scale
        )
        d_keys_acc = (
            d_keys_acc
            + jnp.einsum(
                "hqk,qhd->khd", d_scores_low, query_block, preferred_element_type=jnp.float32
            )
            * score_scale
        )
        d_values_acc = d_values_acc + jnp.einsum(
            "hqk,qhd->khd",
            probs.astype(jnp.bfloat16),
            d_out_block,
            preferred_element_type=jnp.float32,
        )
        return ((d_keys_acc, d_values_acc), d_query_block)

    zeros_acc = jnp.zeros((row_count, heads_here, HEAD), jnp.float32)
    (d_keys, d_values), d_query_blocks = lax.scan(
        backward_block, (zeros_acc, zeros_acc), (query_blocks, seg_blocks, d_att_blocks, log_norms)
    )
    d_queries = d_query_blocks.reshape(row_count, local_cols)
    d_keys = d_keys.reshape(row_count, local_cols)
    d_values = d_values.reshape(row_count, local_cols)
    grad_b_qv = jnp.stack([jnp.sum(d_queries, axis=0), jnp.sum(d_values, axis=0)])
    stacked = jnp.stack([d_queries, d_keys, d_values]).astype(jnp.bfloat16)
    grad_w_qkv = jnp.einsum("td,stc->sdc", normed_one, stacked, preferred_element_type=jnp.float32)
    d_normed_one = lax.psum(
        jnp.einsum("stc,sdc->td", stacked, w_qkv, preferred_element_type=jnp.float32).astype(
            jnp.bfloat16
        ),
        "mp",
    ).astype(jnp.float32)
    d_input_norm, grad_ln1_gain, grad_ln1_bias = norm_one_back(d_normed_one)
    grad_tokens = d_middle + d_input_norm
    summed_qkv, summed_out, summed_fc1, summed_fc2 = (
        lax.psum_scatter(grad_w_qkv, "dp", scatter_dimension=1, tiled=True),
        lax.psum_scatter(grad_w_out, "dp", scatter_dimension=1, tiled=True),
        lax.psum_scatter(grad_w_fc1, "dp", scatter_dimension=0, tiled=True),
        lax.psum_scatter(grad_w_fc2, "dp", scatter_dimension=1, tiled=True),
    )
    small_sums = lax.psum(
        (
            grad_ln1_gain,
            grad_ln1_bias,
            grad_ln2_gain,
            grad_ln2_bias,
            grad_b_out,
            grad_b_fc2,
            grad_b_qv,
            grad_b_fc1,
        ),
        "dp",
    )
    return (
        output,
        grad_tokens,
        summed_qkv,
        small_sums[6],
        summed_out,
        small_sums[4],
        summed_fc1,
        small_sums[7],
        summed_fc2,
        small_sums[5],
        small_sums[0],
        small_sums[1],
        small_sums[2],
        small_sums[3],
    )


def solution(mesh):
    in_specs = (
        P("dp", None),
        P("dp", None),
        P("dp", None),
        P(None, None, "mp"),
        P(None, "mp"),
        P("mp", None),
        P(),
        P(None, "mp"),
        P("mp"),
        P("mp", None),
        P(),
        P(),
        P(),
        P(),
        P(),
    )
    out_specs = (
        P("dp", None),
        P("dp", None),
        P(None, "dp", "mp"),
        P(None, "mp"),
        P("mp", "dp"),
        P(),
        P("dp", "mp"),
        P("mp"),
        P("mp", "dp"),
        P(),
        P(),
        P(),
        P(),
        P(),
    )
    return jax.shard_map(
        per_device, mesh=mesh, in_specs=in_specs, out_specs=out_specs, check_vma=False
    )
```

profile of v0, /device:TPU:0, one launch (start us, length us, event | category | flops | bytes accessed | tf_op | source)
XLA Modules:
  0.0 1066.7 jit_solution(14940275114370547031)
XLA Ops:
  32.3 64.4 %while.27 = (s32[]{:T(128)}, bf16[4,512,4,64]{1,3,2,0:T(8,128)(2,1)}, f32[4,4,512]{2,1,0:T(4,128)}, s32[4,512]{1,0:T(4,128)S(1)}, s32[2048]{0:T(1024)S(1)}, /*in...) while((s32[]{:T(128)}, ...), condition=%wide.region_7.8_spmd, body=%wide.region_4.7_spmd.sunk | while | flops 1125251072 | bytes 61421712 | solution.py:90
  105.5 88.3 %all-reduce.6.cloned.1.call-done = bf16[2048,1024]{1,0:T(8,128)(2,1)} async-done(((bf16[2048,1024]{1,0:T(8,128)(2,1)}), bf16[2048,1024]{1,0:T(8,128)(2,1)}) %all-reduce.6.cloned.1.call-update) | async-done | bytes 4194320 | tf_op jit(solution)/shard_map/psum | solution.py:92
  207.7 25.4 %fusion.94 = (f32[1024]{0:T(1024)}, bf16[2048,1024]{1,0:T(8,128)(2,1)S(1)}, f32[2048,1024]{1,0:T(8,128)}) fusion(f32[2048,1024]{1,0:T(8,128)S(1)} %fusion.91, f32[1024]{0:T(1024)S(1)} %copy-done.52, bf16[2048,1024]{1,0:T(8,128)(2,1)S(1)} %copy-done.21, bf16[1024,1024]{1,0:T(8,128)(2,1)S(1)} %copy-done), kind=kOutput, calls=%fused_computation.147 | convolution fusion | flops 4450155520 | bytes 27271168 | tf_op jit(solution)/shard_map/td,fd->tf/dot_general | solution.py:108
  241.7 10.4 multiply_convert_fusion.1
  252.1 8.4 convolution_convert_fusion.2
  260.5 66.8 %all-reduce.8.cloned.1.call-done = bf16[2048,1024]{1,0:T(8,128)(2,1)} async-done(((bf16[2048,1024]{1,0:T(8,128)(2,1)}), bf16[2048,1024]{1,0:T(8,128)(2,1)}) %all-reduce.8.cloned.1.call-update) | async-done | bytes 4194320 | tf_op jit(solution)/shard_map/psum | solution.py:113
  327.3 8.5 convert_reduce_fusion.1
  360.5 195.5 %while.28 = (s32[]{:T(128)}, f32[2048,4,64]{0,2,1:T(8,128)}, f32[2048,4,64]{0,2,1:T(8,128)}, f32[4,512,4,64]{1,3,2,0:T(8,128)}, bf16[4,512,4,64]{1,3,2,0:T(8,128...) while((s32[]{:T(128)}, f32[2048,4,64]{0,2,1:T(8,128)}, ...), condition=%wide.region_17.18_spmd.clone, body=%wide.region_15.17_spmd.clone.sunk | while | flops 2751068160 | bytes 164206880 | solution.py:159
  373.7 11.5 %multiply_reduce_fusion.3 = (f32[4,512]{1,0:T(4,128)}, f32[4,512,2048]{2,1,0:T(8,128)}) fusion(f32[4,512,2048]{2,1,0:T(8,128)S(1)} %fusion.158, f32[4,512]{1,0:T(4,128)S(1)} %dynamic-slice_bitcast_fusion.2, pred[512,2048]{1,0:T(8,128)(4,1)} %copy-done.8, bf16[2048,4,64]{0,2,1:T(8,128)(2,1)} %get-tuple-element.520, ...), kind=kOutput, calls=%fused_computation.19.clone.1 | convolution fusion | flops 557840384 | bytes 35930116 | tf_op jit(solution)/shard_map/while/body/eval_jaxpr/qhd,khd->hqk/dot_general | solution.py:134
  385.2 11.1 %multiply_convert_fusion.3 = bf16[4,512,2048]{2,1,0:T(8,128)(2,1)} fusion(f32[4,512,2048]{2,1,0:T(8,128)} %get-tuple-element.455, f32[4,512,2048]{2,1,0:T(8,128)S(1)} %fusion.158, f32[4,512]{1,0:T(4,128)} %get-tuple-element.456, f32[4,512]{1,0:T(4,128)S(1)} %dynamic-slice_bitcast_fusion.2, pred[512,2048]{1,0:T(8,128)(4,1)} %copy-done.8), kind=kLoop, calls=%fused_computation.18.clone.1 | loop fusion | flops 25165824 | bytes 43008000 | tf_op jit(solution)/shard_map/while/body/eval_jaxpr/convert_element_type | solution.py:138
  401.6 7.7 fusion.161
  414.9 7.6 fusion.160
  422.5 11.5 %multiply_reduce_fusion.3 = (f32[4,512]{1,0:T(4,128)}, f32[4,512,2048]{2,1,0:T(8,128)}) fusion(f32[4,512,2048]{2,1,0:T(8,128)S(1)} %fusion.158, f32[4,512]{1,0:T(4,128)S(1)} %dynamic-slice_bitcast_fusion.2, pred[512,2048]{1,0:T(8,128)(4,1)} %copy-done.8, bf16[2048,4,64]{0,2,1:T(8,128)(2,1)} %get-tuple-element.520, ...), kind=kOutput, calls=%fused_computation.19.clone.1 | convolution fusion | flops 557840384 | bytes 35930116 | tf_op jit(solution)/shard_map/while/body/eval_jaxpr/qhd,khd->hqk/dot_general | solution.py:134
  434.0 11.1 %multiply_convert_fusion.3 = bf16[4,512,2048]{2,1,0:T(8,128)(2,1)} fusion(f32[4,512,2048]{2,1,0:T(8,128)} %get-tuple-element.455, f32[4,512,2048]{2,1,0:T(8,128)S(1)} %fusion.158, f32[4,512]{1,0:T(4,128)} %get-tuple-element.456, f32[4,512]{1,0:T(4,128)S(1)} %dynamic-slice_bitcast_fusion.2, pred[512,2048]{1,0:T(8,128)(4,1)} %copy-done.8), kind=kLoop, calls=%fused_computation.18.clone.1 | loop fusion | flops 25165824 | bytes 43008000 | tf_op jit(solution)/shard_map/while/body/eval_jaxpr/convert_element_type | solution.py:138
  450.5 7.7 fusion.161
  471.4 11.5 %multiply_reduce_fusion.3 = (f32[4,512]{1,0:T(4,128)}, f32[4,512,2048]{2,1,0:T(8,128)}) fusion(f32[4,512,2048]{2,1,0:T(8,128)S(1)} %fusion.158, f32[4,512]{1,0:T(4,128)S(1)} %dynamic-slice_bitcast_fusion.2, pred[512,2048]{1,0:T(8,128)(4,1)} %copy-done.8, bf16[2048,4,64]{0,2,1:T(8,128)(2,1)} %get-tuple-element.520, ...), kind=kOutput, calls=%fused_computation.19.clone.1 | convolution fusion | flops 557840384 | bytes 35930116 | tf_op jit(solution)/shard_map/while/body/eval_jaxpr/qhd,khd->hqk/dot_general | solution.py:134
  482.9 11.1 %multiply_convert_fusion.3 = bf16[4,512,2048]{2,1,0:T(8,128)(2,1)} fusion(f32[4,512,2048]{2,1,0:T(8,128)} %get-tuple-element.455, f32[4,512,2048]{2,1,0:T(8,128)S(1)} %fusion.158, f32[4,512]{1,0:T(4,128)} %get-tuple-element.456, f32[4,512]{1,0:T(4,128)S(1)} %dynamic-slice_bitcast_fusion.2, pred[512,2048]{1,0:T(8,128)(4,1)} %copy-done.8), kind=kLoop, calls=%fused_computation.18.clone.1 | loop fusion | flops 25165824 | bytes 43008000 | tf_op jit(solution)/shard_map/while/body/eval_jaxpr/convert_element_type | solution.py:138
  499.3 7.7 fusion.161
  512.6 7.6 fusion.160
  520.2 11.5 %multiply_reduce_fusion.3 = (f32[4,512]{1,0:T(4,128)}, f32[4,512,2048]{2,1,0:T(8,128)}) fusion(f32[4,512,2048]{2,1,0:T(8,128)S(1)} %fusion.158, f32[4,512]{1,0:T(4,128)S(1)} %dynamic-slice_bitcast_fusion.2, pred[512,2048]{1,0:T(8,128)(4,1)} %copy-done.8, bf16[2048,4,64]{0,2,1:T(8,128)(2,1)} %get-tuple-element.520, ...), kind=kOutput, calls=%fused_computation.19.clone.1 | convolution fusion | flops 557840384 | bytes 35930116 | tf_op jit(solution)/shard_map/while/body/eval_jaxpr/qhd,khd->hqk/dot_general | solution.py:134
  531.7 11.1 %multiply_convert_fusion.3 = bf16[4,512,2048]{2,1,0:T(8,128)(2,1)} fusion(f32[4,512,2048]{2,1,0:T(8,128)} %get-tuple-element.455, f32[4,512,2048]{2,1,0:T(8,128)S(1)} %fusion.158, f32[4,512]{1,0:T(4,128)} %get-tuple-element.456, f32[4,512]{1,0:T(4,128)S(1)} %dynamic-slice_bitcast_fusion.2, pred[512,2048]{1,0:T(8,128)(4,1)} %copy-done.8), kind=kLoop, calls=%fused_computation.18.clone.1 | loop fusion | flops 25165824 | bytes 43008000 | tf_op jit(solution)/shard_map/while/body/eval_jaxpr/convert_element_type | solution.py:138
  548.1 7.6 fusion.161
  576.8 7.7 fusion.77
  590.3 10.0 fusion.100
  600.7 12.4 %fusion.74 = f32[1024,1024]{1,0:T(8,128)} fusion(bf16[2048,1024]{1,0:T(8,128)(2,1)} %copy-done.57, f32[1024]{0:T(1024)S(1)} %copy-done.56, f32[1024]{0:T(1024)S(1)} %copy-done.44, f32[2048]{0:T(1024)S(1)} %copy-done.38, bf16[2048,1024]{1,0:T(8,128)(2,1)} %all-reduce.6.cloned.1.call-done, bf16[2048,1024]{1,0:T(8,128)(2,1)} %param.19, ...), kind=kOutput, calls=%fused_computation.120 | convolution fusion | flops 4313841664 | bytes 16805888 | tf_op jit(solution)/shard_map/td,tf->df/dot_general | solution.py:112
  613.3 115.5 %all-reduce.10.cloned.1.call-done = (bf16[2048,1024]{1,0:T(8,128)(2,1)}, bf16[2048,1024]{1,0:T(8,128)(2,1)}) async-done(((bf16[2048,1024]{1,0:T(8,128)(2,1)}, bf16[2048,1024]{1,0:T(8,128)(2,1)}), (bf16[2048,1024]{1,0:T(8,128)(2,1)}, bf16[2048,1024]{1,0:T(8,128)(2,1)})) %all-reduce.10.cloned.1.call-update) | async-done | bytes 8388624 | tf_op jit(solution)/shard_map/psum | solution.py:101
  740.2 38.7 %all-reduce = (f32[2,256]{1,0:T(2,128)}, f32[1024]{0:T(1024)}, f32[1024]{0:T(1024)}, f32[1024]{0:T(1024)}, f32[1024]{0:T(1024)}, /*index=5*/f32[1024]{0:T(1024)}, f32[1024]{0:T(1024)}, f32[1024]{0:T(1024)}) all-reduce(f32[2,256]{1,0:T(2,128)S(1)} %pad_maximum_fusion.3, ...), channel_id=1, replica_groups=mesh['dp'=8,'mp'=4] {'dp'}, use_global_device_ids=true, to_apply=%region_24.25 | all-reduce | flops 7680 | bytes 61440 | tf_op jit(solution)/shard_map/psum | solution.py:182
  778.9 16.0 %add_add_fusion.2 = (f32[2048,1024]{1,0:T(8,128)}, bf16[2048,1024]{1,0:T(8,128)(2,1)}) fusion(f32[2048,1024]{1,0:T(8,128)} %copy-done.9, bf16[2048,1024]{1,0:T(8,128)(2,1)} %param.19, bf16[2048,1024]{1,0:T(8,128)(2,1)} %get-tuple-element.311, f32[2048]{0:T(1024)S(1)} %negate_multiply_fusion.1, f32[2048]{0:T(1024)S(1)} %multiply_multiply_fusion.5, ...), kind=kLoop, calls=%fused_computation.83 | loop fusion | flops 35651584 | bytes 37793792 | tf_op jit(solution)/shard_map/add | solution.py:175
  794.9 13.0 %reduce-scatter.5.cloned.1.call-done = f32[3,128,256]{1,2,0:T(8,128)} async-done(((f32[3,1024,256]{1,2,0:T(8,128)}), f32[3,128,256]{1,2,0:T(8,128)}) %reduce-scatter.5.cloned.1.call-update) | async-done | bytes 393232 | tf_op jit(solution)/shard_map/reduce_scatter | solution.py:177
  809.8 65.8 %reduce-scatter.7.cloned.1.call-done = f32[256,128]{1,0:T(8,128)} async-done(((f32[256,1024]{1,0:T(8,128)}), f32[256,128]{1,0:T(8,128)}) %reduce-scatter.7.cloned.1.call-update) | async-done | bytes 131088 | tf_op jit(solution)/shard_map/reduce_scatter | solution.py:178
  875.6 91.7 %reduce-scatter.11.cloned.1.call-done = f32[1024,128]{1,0:T(8,128)} async-done(((f32[1024,1024]{1,0:T(8,128)}), f32[1024,128]{1,0:T(8,128)}) %reduce-scatter.11.cloned.1.call-update) | async-done | bytes 524304 | tf_op jit(solution)/shard_map/reduce_scatter | solution.py:180
  967.3 92.2 %reduce-scatter.9.cloned.1.call-done = f32[128,1024]{1,0:T(8,128)} async-done(((f32[1024,1024]{1,0:T(8,128)}), f32[128,1024]{1,0:T(8,128)}) %reduce-scatter.9.cloned.1.call-update) | async-done | bytes 524304 | tf_op jit(solution)/shard_map/reduce_scatter | solution.py:179
  (258 shorter events, 243.4 us)
Async XLA Ops:
  7.2 200.5 %copy-start = (bf16[1024,1024]{1,0:T(8,128)(2,1)S(1)}, bf16[1024,1024]{1,0:T(8,128)(2,1)}, u32[]{:S(2)}) copy-start(bf16[1024,1024]{1,0:T(8,128)(2,1)} %param.28) | copy-start | bytes 6291460
  7.2 186.6 %all-reduce.6.cloned.1.call-start = ((), (), s32[]{:S(2)}) async-start(), calls=%async_computation.4 | async-start | bytes 8388608 | tf_op jit(solution)/shard_map/psum | solution.py:92
  97.3 96.4 %copy-start.32 = (f32[1024]{0:T(1024)S(1)}, f32[1024]{0:T(1024)}, u32[]{:S(2)}) copy-start(f32[1024]{0:T(1024)} %param.25) | copy-start | bytes 12292
  105.4 96.4 %copy-start.43 = (f32[1024]{0:T(1024)S(1)}, f32[1024]{0:T(1024)}, u32[]{:S(2)}) copy-start(f32[1024]{0:T(1024)} %param.32) | copy-start | bytes 12292
  105.4 96.4 %copy-start.55 = (f32[1024]{0:T(1024)S(1)}, f32[1024]{0:T(1024)}, u32[]{:S(2)}) copy-start(f32[1024]{0:T(1024)} %param.33) | copy-start | bytes 12292
  105.5 221.8 %all-reduce.8.cloned.1.call-start = ((), (), s32[]{:S(2)}) async-start(), calls=%async_computation.5 | async-start | bytes 8388608 | tf_op jit(solution)/shard_map/psum | solution.py:113
  199.7 143.1 %copy-start.30 = (f32[2048]{0:T(1024)}, f32[2048]{0:T(1024)S(1)}, u32[]{:S(2)}) copy-start(f32[2048]{0:T(1024)S(1)} %broadcast_multiply_fusion) | copy-start | bytes 24580
  201.8 140.9 %copy-start.37 = (f32[2048]{0:T(1024)}, f32[2048]{0:T(1024)S(1)}, u32[]{:S(2)}) copy-start(f32[2048]{0:T(1024)S(1)} %fusion.87) | copy-start | bytes 24580
  207.7 25.4 %copy-start.19 = (f32[2048,1024]{1,0:T(8,128)}, f32[2048,1024]{1,0:T(8,128)S(1)}, u32[]{:S(2)}) copy-start(f32[2048,1024]{1,0:T(8,128)S(1)} %fusion.91) | copy-start | bytes 25165828
  241.5 487.3 %all-reduce.10.cloned.1.call-start = ((), (), s32[]{:S(2)}) async-start(), calls=%async_computation.10 | async-start | bytes 16777216 | tf_op jit(solution)/shard_map/psum | solution.py:101
  385.2 11.1 %copy-start.12 = (f32[2048,4,64]{0,2,1:T(8,128)S(1)}, f32[2048,4,64]{0,2,1:T(8,128)}, u32[]{:S(2)}) copy-start(f32[2048,4,64]{0,2,1:T(8,128)} %get-tuple-element.498) | copy-start | bytes 6291460 | tf_op jit(solution)/shard_map/while
  396.3 13.0 %copy-start.26 = (s32[2048]{0:T(1024)S(1)}, s32[2048]{0:T(1024)}, u32[]{:S(2)}) copy-start(s32[2048]{0:T(1024)} %get-tuple-element.570) | copy-start | bytes 24580 | tf_op jit(solution)/shard_map/while
  445.1 13.0 %copy-start.26 = (s32[2048]{0:T(1024)S(1)}, s32[2048]{0:T(1024)}, u32[]{:S(2)}) copy-start(s32[2048]{0:T(1024)} %get-tuple-element.570) | copy-start | bytes 24580 | tf_op jit(solution)/shard_map/while
  482.8 11.1 %copy-start.12 = (f32[2048,4,64]{0,2,1:T(8,128)S(1)}, f32[2048,4,64]{0,2,1:T(8,128)}, u32[]{:S(2)}) copy-start(f32[2048,4,64]{0,2,1:T(8,128)} %get-tuple-element.498) | copy-start | bytes 6291460 | tf_op jit(solution)/shard_map/while
  494.0 13.0 %copy-start.26 = (s32[2048]{0:T(1024)S(1)}, s32[2048]{0:T(1024)}, u32[]{:S(2)}) copy-start(s32[2048]{0:T(1024)} %get-tuple-element.570) | copy-start | bytes 24580 | tf_op jit(solution)/shard_map/while
  531.7 11.1 %copy-start.12 = (f32[2048,4,64]{0,2,1:T(8,128)S(1)}, f32[2048,4,64]{0,2,1:T(8,128)}, u32[]{:S(2)}) copy-start(f32[2048,4,64]{0,2,1:T(8,128)} %get-tuple-element.498) | copy-start | bytes 6291460 | tf_op jit(solution)/shard_map/while
  542.8 13.0 %copy-start.26 = (s32[2048]{0:T(1024)S(1)}, s32[2048]{0:T(1024)}, u32[]{:S(2)}) copy-start(s32[2048]{0:T(1024)} %get-tuple-element.570) | copy-start | bytes 24580 | tf_op jit(solution)/shard_map/while
  575.6 232.3 %reduce-scatter.5.cloned.1.call-start = ((), (), s32[]{:S(2)}) async-start(), calls=%async_computation.6 | async-start | bytes 3538944 | tf_op jit(solution)/shard_map/reduce_scatter | solution.py:177
  584.5 291.1 %reduce-scatter.7.cloned.1.call-start = ((), (), s32[]{:S(2)}) async-start(), calls=%async_computation.7 | async-start | bytes 1179648 | tf_op jit(solution)/shard_map/reduce_scatter | solution.py:178
  590.3 377.0 %reduce-scatter.11.cloned.1.call-start = ((), (), s32[]{:S(2)}) async-start(), calls=%async_computation.9 | async-start | bytes 4718592 | tf_op jit(solution)/shard_map/reduce_scatter | solution.py:180
  600.3 128.5 %copy-start.29 = (f32[2048]{0:T(1024)S(1)}, f32[2048]{0:T(1024)}, u32[]{:S(2)}) copy-start(f32[2048]{0:T(1024)} %copy-done.28) | copy-start | bytes 24580
  600.4 128.5 %copy-start.42 = (f32[1024]{0:T(1024)S(1)}, f32[1024]{0:T(1024)}, u32[]{:S(2)}) copy-start(f32[1024]{0:T(1024)} %param.30) | copy-start | bytes 12292
  600.4 459.1 %reduce-scatter.9.cloned.1.call-start = ((), (), s32[]{:S(2)}) async-start(), calls=%async_computation.8 | async-start | bytes 4718592 | tf_op jit(solution)/shard_map/reduce_scatter | solution.py:179
  613.1 121.4 %copy-start.40 = (f32[2048]{0:T(1024)S(1)}, f32[2048]{0:T(1024)}, u32[]{:S(2)}) copy-start(f32[2048]{0:T(1024)} %copy-done.39) | copy-start | bytes 24580
  613.1 121.5 %copy-start.35 = (f32[2048]{0:T(1024)S(1)}, f32[2048]{0:T(1024)}, u32[]{:S(2)}) copy-start(f32[2048]{0:T(1024)} %copy-done.34) | copy-start | bytes 24580
  728.8 11.3 %copy-start.45 = (f32[1024]{0:T(1024)S(1)}, f32[1024]{0:T(1024)}, u32[]{:S(2)}) copy-start(f32[1024]{0:T(1024)} %get-tuple-element.260) | copy-start | bytes 12292
  728.8 11.3 %copy-start.46 = (f32[1024]{0:T(1024)S(1)}, f32[1024]{0:T(1024)}, u32[]{:S(2)}) copy-start(f32[1024]{0:T(1024)} %get-tuple-element.256) | copy-start | bytes 12292
  728.8 11.3 %copy-start.47 = (f32[1024]{0:T(1024)S(1)}, f32[1024]{0:T(1024)}, u32[]{:S(2)}) copy-start(f32[1024]{0:T(1024)} %get-tuple-element.315) | copy-start | bytes 12292
  728.8 11.3 %copy-start.48 = (f32[1024]{0:T(1024)S(1)}, f32[1024]{0:T(1024)}, u32[]{:S(2)}) copy-start(f32[1024]{0:T(1024)} %get-tuple-element.321) | copy-start | bytes 12292
  728.9 11.3 %copy-start.51 = (f32[1024]{0:T(1024)S(1)}, f32[1024]{0:T(1024)}, u32[]{:S(2)}) copy-start(f32[1024]{0:T(1024)} %get-tuple-element.312) | copy-start | bytes 12292
  728.9 50.0 %copy-start.50 = (f32[1024]{0:T(1024)S(1)}, f32[1024]{0:T(1024)}, u32[]{:S(2)}) copy-start(f32[1024]{0:T(1024)} %param.29) | copy-start | bytes 12292
  778.9 280.6 %copy-start.1 = (bf16[1024,1024]{1,0:T(8,128)(2,1)S(1)}, bf16[1024,1024]{1,0:T(8,128)(2,1)}, u32[]{:S(2)}) copy-start(bf16[1024,1024]{1,0:T(8,128)(2,1)} %param.28) | copy-start | bytes 6291460
  (48 other events, 301.6 us)
Sparse Core Ops, SparseCore 0:
  105.5 88.1 all-reduce.5
  241.6 85.6 all-reduce.7
  575.7 153.0 all-reduce.9
  732.3 75.5 reduce-scatter.4
  811.7 63.8 reduce-scatter.6
  879.6 87.6 reduce-scatter.10
  971.5 87.9 reduce-scatter.8
where the time goes:
time: 1080 us; the launch traced here: 1070 us
  waiting for transfers between devices  533 us (49%)
  matrix products  285 us (26%)
  other arithmetic  151 us (14%)
  local copies, waits for them, and re-layouts  41.2 us (4%)
  blocking collectives  38.7 us (4%)
  between operations  15.2 us (1%)
    psum x1, waiting for transfers between devices, per_device(): lax.psum(jnp.dot(activated, w_fc2, preferred_element_type=jnp.float32).as...  115 us
    reduce_scatter x1, waiting for transfers between devices, per_device(): lax.psum_scatter(grad_w_fc1, 'dp', scatter_dimension=0, tiled=True)  92.2 us
    reduce_scatter x1, waiting for transfers between devices, per_device(): lax.psum_scatter(grad_w_fc2, 'dp', scatter_dimension=1, tiled=True)  91.7 us
    psum x1, waiting for transfers between devices, per_device(): lax.psum(jnp.dot(attended, w_out, preferred_element_type=jnp.float32).ast...  88.3 us
    psum x1, waiting for transfers between devices, per_device(): lax.psum(jnp.einsum('tf,df->td', d_pre_low, w_fc1, preferred_element_type...  66.8 us
    reduce_scatter x1, waiting for transfers between devices, per_device(): lax.psum_scatter(grad_w_out, 'dp', scatter_dimension=1, tiled=True)  65.8 us
    dot_general x4, matrix products, backward_block(): jnp.einsum('qhd,khd->hqk', d_out_block, value_heads, preferred_element_ty...  45.9 us
    convert_element_type x4, other arithmetic, backward_block(): d_scores_low = d_scores.astype(jnp.bfloat16)  44.5 us
  transfers between devices with their start and end apart: 7, of which 7 were waited for; matrix products, arithmetic and copies ran while one was open for 8% of the time, Pallas kernels for 0%

commit v1 on v0

--- a/solution.py
+++ b/solution.py
@@ -110,11 +110,14 @@
     grad_b_fc1 = jnp.sum(d_pre, axis=0)
     d_pre_low = d_pre.astype(jnp.bfloat16)
     grad_w_fc1 = jnp.einsum("td,tf->df", normed_two, d_pre_low, preferred_element_type=jnp.float32)
-    d_normed_two = lax.psum(
-        jnp.einsum("tf,df->td", d_pre_low, w_fc1, preferred_element_type=jnp.float32).astype(
-            jnp.bfloat16
+    d_normed_two = jnp.sum(
+        lax.all_gather(
+            jnp.einsum("tf,df->td", d_pre_low, w_fc1, preferred_element_type=jnp.float32).astype(
+                jnp.bfloat16
+            ),
+            "mp",
         ),
-        "mp",
+        axis=0,
     ).astype(jnp.float32)
     d_middle_norm, grad_ln2_gain, grad_ln2_bias = norm_two_back(d_normed_two)
     d_middle = upstream + d_middle_norm

time: 1080 us -> 1110 us (1.028)
  waiting for transfers between devices: 533 us -> 553 us
  other arithmetic: 151 us -> 163 us
    all_gather x0 -> x1, waiting for transfers between devices: none -> 86.2 us  [per_device(): lax.all_gather(jnp.einsum('tf,df->td', d_pre_low, w_fc1, preferred_elemen...]
    psum x1 -> x0, waiting for transfers between devices: 66.8 us -> none  [per_device(): lax.psum(jnp.einsum('tf,df->td', d_pre_low, w_fc1, preferred_element_type...]
    reduce_sum x0 -> x1, other arithmetic: none -> 12.1 us  [per_device(): jnp.sum(lax.all_gather(jnp.einsum('tf,df->td', d_pre_low, w_fc1, preferre...]
where the time goes in v1:
time: 1110 us; the launch traced here: 1100 us
  waiting for transfers between devices  553 us (50%)
  matrix products  286 us (26%)
  other arithmetic  163 us (15%)
  local copies, waits for them, and re-layouts  41.7 us (4%)
  blocking collectives  38.5 us (3%)
  between operations  15 us (1%)
    psum x1, waiting for transfers between devices, per_device(): lax.psum(jnp.dot(activated, w_fc2, preferred_element_type=jnp.float32).as...  115 us
    reduce_scatter x1, waiting for transfers between devices, per_device(): lax.psum_scatter(grad_w_fc1, 'dp', scatter_dimension=0, tiled=True)  92 us
    reduce_scatter x1, waiting for transfers between devices, per_device(): lax.psum_scatter(grad_w_fc2, 'dp', scatter_dimension=1, tiled=True)  90 us
    psum x1, waiting for transfers between devices, per_device(): lax.psum(jnp.dot(attended, w_out, preferred_element_type=jnp.float32).ast...  88.3 us
    all_gather x1, waiting for transfers between devices, per_device(): lax.all_gather(jnp.einsum('tf,df->td', d_pre_low, w_fc1, preferred_elemen...  86.2 us
    reduce_scatter x1, waiting for transfers between devices, per_device(): lax.psum_scatter(grad_w_out, 'dp', scatter_dimension=1, tiled=True)  68.3 us
    dot_general x4, matrix products, backward_block(): jnp.einsum('qhd,khd->hqk', d_out_block, value_heads, preferred_element_ty...  45.9 us
    convert_element_type x4, other arithmetic, backward_block(): d_scores_low = d_scores.astype(jnp.bfloat16)  44.4 us
  transfers between devices with their start and end apart: 7, of which 7 were waited for; matrix products, arithmetic and copies ran while one was open for 8% of the time, Pallas kernels for 0%

profile of v1, /device:TPU:0, one launch (start us, length us, event | category | flops | bytes accessed | tf_op | source)
XLA Modules:
  0.0 1099.3 jit_solution(10294894990419660007)
XLA Ops:
  32.3 64.2 %while.27 = (s32[]{:T(128)}, bf16[4,512,4,64]{1,3,2,0:T(8,128)(2,1)}, f32[4,4,512]{2,1,0:T(4,128)}, s32[4,512]{1,0:T(4,128)S(1)}, s32[2048]{0:T(1024)S(1)}, /*in...) while((s32[]{:T(128)}, ...), condition=%wide.region_7.8_spmd, body=%wide.region_4.7_spmd.sunk | while | flops 1125251072 | bytes 61421712 | solution.py:90
  105.3 88.3 %all-reduce.5.cloned.1.call-done = bf16[2048,1024]{1,0:T(8,128)(2,1)} async-done(((bf16[2048,1024]{1,0:T(8,128)(2,1)}), bf16[2048,1024]{1,0:T(8,128)(2,1)}) %all-reduce.5.cloned.1.call-update) | async-done | bytes 4194320 | tf_op jit(solution)/shard_map/psum | solution.py:92
  207.5 25.4 %fusion.94 = (f32[1024]{0:T(1024)}, bf16[2048,1024]{1,0:T(8,128)(2,1)S(1)}, f32[2048,1024]{1,0:T(8,128)}) fusion(f32[2048,1024]{1,0:T(8,128)S(1)} %fusion.91, f32[1024]{0:T(1024)S(1)} %copy-done.53, bf16[2048,1024]{1,0:T(8,128)(2,1)S(1)} %copy-done.21, bf16[1024,1024]{1,0:T(8,128)(2,1)S(1)} %copy-done), kind=kOutput, calls=%fused_computation.147 | convolution fusion | flops 4450155520 | bytes 27271168 | tf_op jit(solution)/shard_map/td,fd->tf/dot_general | solution.py:108
  241.8 10.5 multiply_convert_fusion.1
  252.3 9.0 convolution_convert_fusion.2
  261.3 86.2 %all-gather.3.cloned.1.call-done = bf16[8192,1024]{1,0:T(8,128)(2,1)} async-done(((bf16[2048,1024]{1,0:T(8,128)(2,1)}), bf16[8192,1024]{1,0:T(8,128)(2,1)}) %all-gather.3.cloned.1.call-update) | async-done | bytes 16777232 | tf_op jit(solution)/shard_map/all_gather | solution.py:114
  347.5 12.1 %reduce_sum.199 = bf16[2048,1024]{1,0:T(8,128)(2,1)} reduce(bf16[4,2048,1024]{2,1,0:T(8,128)(2,1)} %bitcast.142, bf16[]{:T(256)} %constant.63.clone.1), dimensions={0}, to_apply=%region_12.13 | reduce | flops 6291456 | bytes 20971522 | tf_op jit(solution)/shard_map/reduce_sum | solution.py:113
  359.6 8.1 convert_reduce_fusion.1
  392.6 195.2 %while.28 = (s32[]{:T(128)}, f32[2048,4,64]{0,2,1:T(8,128)}, f32[2048,4,64]{0,2,1:T(8,128)}, f32[4,512,4,64]{1,3,2,0:T(8,128)}, bf16[4,512,4,64]{1,3,2,0:T(8,128...) while((s32[]{:T(128)}, f32[2048,4,64]{0,2,1:T(8,128)}, ...), condition=%wide.region_17.18_spmd.clone, body=%wide.region_15.17_spmd.clone.sunk | while | flops 2751068160 | bytes 164206880 | solution.py:162
  405.6 11.5 %multiply_reduce_fusion.3 = (f32[4,512]{1,0:T(4,128)}, f32[4,512,2048]{2,1,0:T(8,128)}) fusion(f32[4,512,2048]{2,1,0:T(8,128)S(1)} %fusion.158, f32[4,512]{1,0:T(4,128)S(1)} %dynamic-slice_bitcast_fusion.2, pred[512,2048]{1,0:T(8,128)(4,1)} %copy-done.8, bf16[2048,4,64]{0,2,1:T(8,128)(2,1)} %get-tuple-element.520, ...), kind=kOutput, calls=%fused_computation.19.clone.1 | convolution fusion | flops 557840384 | bytes 35930116 | tf_op jit(solution)/shard_map/while/body/eval_jaxpr/qhd,khd->hqk/dot_general | solution.py:137
  417.1 11.1 %multiply_convert_fusion.3 = bf16[4,512,2048]{2,1,0:T(8,128)(2,1)} fusion(f32[4,512,2048]{2,1,0:T(8,128)} %get-tuple-element.455, f32[4,512,2048]{2,1,0:T(8,128)S(1)} %fusion.158, f32[4,512]{1,0:T(4,128)} %get-tuple-element.456, f32[4,512]{1,0:T(4,128)S(1)} %dynamic-slice_bitcast_fusion.2, pred[512,2048]{1,0:T(8,128)(4,1)} %copy-done.8), kind=kLoop, calls=%fused_computation.18.clone.1 | loop fusion | flops 25165824 | bytes 43008000 | tf_op jit(solution)/shard_map/while/body/eval_jaxpr/convert_element_type | solution.py:141
  433.5 7.6 fusion.161
  454.4 11.5 %multiply_reduce_fusion.3 = (f32[4,512]{1,0:T(4,128)}, f32[4,512,2048]{2,1,0:T(8,128)}) fusion(f32[4,512,2048]{2,1,0:T(8,128)S(1)} %fusion.158, f32[4,512]{1,0:T(4,128)S(1)} %dynamic-slice_bitcast_fusion.2, pred[512,2048]{1,0:T(8,128)(4,1)} %copy-done.8, bf16[2048,4,64]{0,2,1:T(8,128)(2,1)} %get-tuple-element.520, ...), kind=kOutput, calls=%fused_computation.19.clone.1 | convolution fusion | flops 557840384 | bytes 35930116 | tf_op jit(solution)/shard_map/while/body/eval_jaxpr/qhd,khd->hqk/dot_general | solution.py:137
  465.9 11.1 %multiply_convert_fusion.3 = bf16[4,512,2048]{2,1,0:T(8,128)(2,1)} fusion(f32[4,512,2048]{2,1,0:T(8,128)} %get-tuple-element.455, f32[4,512,2048]{2,1,0:T(8,128)S(1)} %fusion.158, f32[4,512]{1,0:T(4,128)} %get-tuple-element.456, f32[4,512]{1,0:T(4,128)S(1)} %dynamic-slice_bitcast_fusion.2, pred[512,2048]{1,0:T(8,128)(4,1)} %copy-done.8), kind=kLoop, calls=%fused_computation.18.clone.1 | loop fusion | flops 25165824 | bytes 43008000 | tf_op jit(solution)/shard_map/while/body/eval_jaxpr/convert_element_type | solution.py:141
  482.3 7.7 fusion.161
  495.6 7.6 fusion.160
  503.2 11.5 %multiply_reduce_fusion.3 = (f32[4,512]{1,0:T(4,128)}, f32[4,512,2048]{2,1,0:T(8,128)}) fusion(f32[4,512,2048]{2,1,0:T(8,128)S(1)} %fusion.158, f32[4,512]{1,0:T(4,128)S(1)} %dynamic-slice_bitcast_fusion.2, pred[512,2048]{1,0:T(8,128)(4,1)} %copy-done.8, bf16[2048,4,64]{0,2,1:T(8,128)(2,1)} %get-tuple-element.520, ...), kind=kOutput, calls=%fused_computation.19.clone.1 | convolution fusion | flops 557840384 | bytes 35930116 | tf_op jit(solution)/shard_map/while/body/eval_jaxpr/qhd,khd->hqk/dot_general | solution.py:137
  514.7 11.1 %multiply_convert_fusion.3 = bf16[4,512,2048]{2,1,0:T(8,128)(2,1)} fusion(f32[4,512,2048]{2,1,0:T(8,128)} %get-tuple-element.455, f32[4,512,2048]{2,1,0:T(8,128)S(1)} %fusion.158, f32[4,512]{1,0:T(4,128)} %get-tuple-element.456, f32[4,512]{1,0:T(4,128)S(1)} %dynamic-slice_bitcast_fusion.2, pred[512,2048]{1,0:T(8,128)(4,1)} %copy-done.8), kind=kLoop, calls=%fused_computation.18.clone.1 | loop fusion | flops 25165824 | bytes 43008000 | tf_op jit(solution)/shard_map/while/body/eval_jaxpr/convert_element_type | solution.py:141
  531.1 7.7 fusion.161
  544.4 7.6 fusion.160
  552.0 11.5 %multiply_reduce_fusion.3 = (f32[4,512]{1,0:T(4,128)}, f32[4,512,2048]{2,1,0:T(8,128)}) fusion(f32[4,512,2048]{2,1,0:T(8,128)S(1)} %fusion.158, f32[4,512]{1,0:T(4,128)S(1)} %dynamic-slice_bitcast_fusion.2, pred[512,2048]{1,0:T(8,128)(4,1)} %copy-done.8, bf16[2048,4,64]{0,2,1:T(8,128)(2,1)} %get-tuple-element.520, ...), kind=kOutput, calls=%fused_computation.19.clone.1 | convolution fusion | flops 557840384 | bytes 35930116 | tf_op jit(solution)/shard_map/while/body/eval_jaxpr/qhd,khd->hqk/dot_general | solution.py:137
  563.5 11.1 %multiply_convert_fusion.3 = bf16[4,512,2048]{2,1,0:T(8,128)(2,1)} fusion(f32[4,512,2048]{2,1,0:T(8,128)} %get-tuple-element.455, f32[4,512,2048]{2,1,0:T(8,128)S(1)} %fusion.158, f32[4,512]{1,0:T(4,128)} %get-tuple-element.456, f32[4,512]{1,0:T(4,128)S(1)} %dynamic-slice_bitcast_fusion.2, pred[512,2048]{1,0:T(8,128)(4,1)} %copy-done.8), kind=kLoop, calls=%fused_computation.18.clone.1 | loop fusion | flops 25165824 | bytes 43008000 | tf_op jit(solution)/shard_map/while/body/eval_jaxpr/convert_element_type | solution.py:141
  580.0 7.6 fusion.161
  616.8 10.0 fusion.100
  627.0 12.5 %fusion.74 = f32[1024,1024]{1,0:T(8,128)} fusion(bf16[2048,1024]{1,0:T(8,128)(2,1)} %copy-done.58, f32[1024]{0:T(1024)S(1)} %copy-done.57, f32[1024]{0:T(1024)S(1)} %copy-done.45, f32[2048]{0:T(1024)S(1)} %copy-done.39, bf16[2048,1024]{1,0:T(8,128)(2,1)} %all-reduce.5.cloned.1.call-done, bf16[2048,1024]{1,0:T(8,128)(2,1)} %param.19, ...), kind=kOutput, calls=%fused_computation.120 | convolution fusion | flops 4313841664 | bytes 16805888 | tf_op jit(solution)/shard_map/td,tf->df/dot_general | solution.py:112
  645.9 114.6 %all-reduce.7.cloned.1.call-done = (bf16[2048,1024]{1,0:T(8,128)(2,1)}, bf16[2048,1024]{1,0:T(8,128)(2,1)}) async-done(((bf16[2048,1024]{1,0:T(8,128)(2,1)}, bf16[2048,1024]{1,0:T(8,128)(2,1)}), (bf16[2048,1024]{1,0:T(8,128)(2,1)}, bf16[2048,1024]{1,0:T(8,128)(2,1)})) %all-reduce.7.cloned.1.call-update) | async-done | bytes 8388624 | tf_op jit(solution)/shard_map/psum | solution.py:101
  771.9 38.5 %all-reduce = (f32[2,256]{1,0:T(2,128)}, f32[1024]{0:T(1024)}, f32[1024]{0:T(1024)}, f32[1024]{0:T(1024)}, f32[1024]{0:T(1024)}, /*index=5*/f32[1024]{0:T(1024)}, f32[1024]{0:T(1024)}, f32[1024]{0:T(1024)}) all-reduce(f32[2,256]{1,0:T(2,128)S(1)} %pad_maximum_fusion.3, ...), channel_id=1, replica_groups=mesh['dp'=8,'mp'=4] {'dp'}, use_global_device_ids=true, to_apply=%region_24.25 | all-reduce | flops 7680 | bytes 61440 | tf_op jit(solution)/shard_map/psum | solution.py:185
  810.4 16.0 %add_add_fusion.2 = (f32[2048,1024]{1,0:T(8,128)}, bf16[2048,1024]{1,0:T(8,128)(2,1)}) fusion(f32[2048,1024]{1,0:T(8,128)} %copy-done.9, bf16[2048,1024]{1,0:T(8,128)(2,1)} %param.19, bf16[2048,1024]{1,0:T(8,128)(2,1)} %get-tuple-element.311, f32[2048]{0:T(1024)S(1)} %negate_multiply_fusion.1, f32[2048]{0:T(1024)S(1)} %multiply_multiply_fusion.5, ...), kind=kLoop, calls=%fused_computation.83 | loop fusion | flops 35651584 | bytes 37793792 | tf_op jit(solution)/shard_map/add | solution.py:178
  826.5 13.6 %reduce-scatter.5.cloned.1.call-done = f32[3,128,256]{1,2,0:T(8,128)} async-done(((f32[3,1024,256]{1,2,0:T(8,128)}), f32[3,128,256]{1,2,0:T(8,128)}) %reduce-scatter.5.cloned.1.call-update) | async-done | bytes 393232 | tf_op jit(solution)/shard_map/reduce_scatter | solution.py:180
  841.9 90.0 %reduce-scatter.11.cloned.1.call-done = f32[1024,128]{1,0:T(8,128)} async-done(((f32[1024,1024]{1,0:T(8,128)}), f32[1024,128]{1,0:T(8,128)}) %reduce-scatter.11.cloned.1.call-update) | async-done | bytes 524304 | tf_op jit(solution)/shard_map/reduce_scatter | solution.py:183
  931.9 92.0 %reduce-scatter.9.cloned.1.call-done = f32[128,1024]{1,0:T(8,128)} async-done(((f32[1024,1024]{1,0:T(8,128)}), f32[128,1024]{1,0:T(8,128)}) %reduce-scatter.9.cloned.1.call-update) | async-done | bytes 524304 | tf_op jit(solution)/shard_map/reduce_scatter | solution.py:182
  1023.9 68.3 %reduce-scatter.7.cloned.1.call-done = f32[256,128]{1,0:T(8,128)} async-done(((f32[256,1024]{1,0:T(8,128)}), f32[256,128]{1,0:T(8,128)}) %reduce-scatter.7.cloned.1.call-update) | async-done | bytes 131088 | tf_op jit(solution)/shard_map/reduce_scatter | solution.py:181
  (261 shorter events, 252.0 us)
Async XLA Ops:
  7.2 200.3 %copy-start = (bf16[1024,1024]{1,0:T(8,128)(2,1)S(1)}, bf16[1024,1024]{1,0:T(8,128)(2,1)}, u32[]{:S(2)}) copy-start(bf16[1024,1024]{1,0:T(8,128)(2,1)} %param.28) | copy-start | bytes 6291460
  7.2 186.4 %all-reduce.5.cloned.1.call-start = ((), (), s32[]{:S(2)}) async-start(), calls=%async_computation.4 | async-start | bytes 8388608 | tf_op jit(solution)/shard_map/psum | solution.py:92
  97.2 96.4 %copy-start.33 = (f32[1024]{0:T(1024)S(1)}, f32[1024]{0:T(1024)}, u32[]{:S(2)}) copy-start(f32[1024]{0:T(1024)} %param.25) | copy-start | bytes 12292
  105.3 96.4 %copy-start.44 = (f32[1024]{0:T(1024)S(1)}, f32[1024]{0:T(1024)}, u32[]{:S(2)}) copy-start(f32[1024]{0:T(1024)} %param.32) | copy-start | bytes 12292
  105.3 96.4 %copy-start.56 = (f32[1024]{0:T(1024)S(1)}, f32[1024]{0:T(1024)}, u32[]{:S(2)}) copy-start(f32[1024]{0:T(1024)} %param.33) | copy-start | bytes 12292
  105.3 242.2 %all-gather.3.cloned.1.call-start = ((), (), s32[]{:S(2)}) async-start(), calls=%async_computation.9 | async-start | bytes 20971520 | tf_op jit(solution)/shard_map/all_gather | solution.py:114
  199.5 175.4 %copy-start.31 = (f32[2048]{0:T(1024)}, f32[2048]{0:T(1024)S(1)}, u32[]{:S(2)}) copy-start(f32[2048]{0:T(1024)S(1)} %broadcast_multiply_fusion) | copy-start | bytes 24580
  201.7 173.2 %copy-start.38 = (f32[2048]{0:T(1024)}, f32[2048]{0:T(1024)S(1)}, u32[]{:S(2)}) copy-start(f32[2048]{0:T(1024)S(1)} %fusion.87) | copy-start | bytes 24580
  207.5 25.4 %copy-start.19 = (f32[2048,1024]{1,0:T(8,128)}, f32[2048,1024]{1,0:T(8,128)S(1)}, u32[]{:S(2)}) copy-start(f32[2048,1024]{1,0:T(8,128)S(1)} %fusion.91) | copy-start | bytes 25165828
  241.3 519.2 %all-reduce.7.cloned.1.call-start = ((), (), s32[]{:S(2)}) async-start(), calls=%async_computation.10 | async-start | bytes 16777216 | tf_op jit(solution)/shard_map/psum | solution.py:101
  417.1 11.1 %copy-start.12 = (f32[2048,4,64]{0,2,1:T(8,128)S(1)}, f32[2048,4,64]{0,2,1:T(8,128)}, u32[]{:S(2)}) copy-start(f32[2048,4,64]{0,2,1:T(8,128)} %get-tuple-element.498) | copy-start | bytes 6291460 | tf_op jit(solution)/shard_map/while
  428.2 13.0 %copy-start.26 = (s32[2048]{0:T(1024)S(1)}, s32[2048]{0:T(1024)}, u32[]{:S(2)}) copy-start(s32[2048]{0:T(1024)} %get-tuple-element.570) | copy-start | bytes 24580 | tf_op jit(solution)/shard_map/while
  465.9 11.1 %copy-start.12 = (f32[2048,4,64]{0,2,1:T(8,128)S(1)}, f32[2048,4,64]{0,2,1:T(8,128)}, u32[]{:S(2)}) copy-start(f32[2048,4,64]{0,2,1:T(8,128)} %get-tuple-element.498) | copy-start | bytes 6291460 | tf_op jit(solution)/shard_map/while
  477.0 13.0 %copy-start.26 = (s32[2048]{0:T(1024)S(1)}, s32[2048]{0:T(1024)}, u32[]{:S(2)}) copy-start(s32[2048]{0:T(1024)} %get-tuple-element.570) | copy-start | bytes 24580 | tf_op jit(solution)/shard_map/while
  525.8 13.0 %copy-start.26 = (s32[2048]{0:T(1024)S(1)}, s32[2048]{0:T(1024)}, u32[]{:S(2)}) copy-start(s32[2048]{0:T(1024)} %get-tuple-element.570) | copy-start | bytes 24580 | tf_op jit(solution)/shard_map/while
  574.6 13.0 %copy-start.26 = (s32[2048]{0:T(1024)S(1)}, s32[2048]{0:T(1024)}, u32[]{:S(2)}) copy-start(s32[2048]{0:T(1024)} %get-tuple-element.570) | copy-start | bytes 24580 | tf_op jit(solution)/shard_map/while
  607.5 232.6 %reduce-scatter.5.cloned.1.call-start = ((), (), s32[]{:S(2)}) async-start(), calls=%async_computation.5 | async-start | bytes 3538944 | tf_op jit(solution)/shard_map/reduce_scatter | solution.py:180
  616.4 315.5 %reduce-scatter.11.cloned.1.call-start = ((), (), s32[]{:S(2)}) async-start(), calls=%async_computation.8 | async-start | bytes 4718592 | tf_op jit(solution)/shard_map/reduce_scatter | solution.py:183
  626.9 13.0 %copy-start.18 = (bf16[32,8,4,512]{3,1,2,0:T(8,128)(2,1)S(1)}, bf16[32,8,4,512]{3,1,2,0:T(8,128)(2,1)}, u32[]{:S(2)}) copy-start(bf16[32,8,4,512]{3,1,2,0:T(8,128)(2,1)} %copy-done.17) | copy-start | bytes 3145732
  626.9 397.1 %reduce-scatter.9.cloned.1.call-start = ((), (), s32[]{:S(2)}) async-start(), calls=%async_computation.7 | async-start | bytes 4718592 | tf_op jit(solution)/shard_map/reduce_scatter | solution.py:182
  639.5 121.0 %copy-start.30 = (f32[2048]{0:T(1024)S(1)}, f32[2048]{0:T(1024)}, u32[]{:S(2)}) copy-start(f32[2048]{0:T(1024)} %copy-done.29) | copy-start | bytes 24580
  639.5 121.0 %copy-start.43 = (f32[1024]{0:T(1024)S(1)}, f32[1024]{0:T(1024)}, u32[]{:S(2)}) copy-start(f32[1024]{0:T(1024)} %param.30) | copy-start | bytes 12292
  639.5 452.7 %reduce-scatter.7.cloned.1.call-start = ((), (), s32[]{:S(2)}) async-start(), calls=%async_computation.6 | async-start | bytes 1179648 | tf_op jit(solution)/shard_map/reduce_scatter | solution.py:181
  639.9 126.4 %copy-start.41 = (f32[2048]{0:T(1024)S(1)}, f32[2048]{0:T(1024)}, u32[]{:S(2)}) copy-start(f32[2048]{0:T(1024)} %copy-done.40) | copy-start | bytes 24580
  639.9 126.4 %copy-start.36 = (f32[2048]{0:T(1024)S(1)}, f32[2048]{0:T(1024)}, u32[]{:S(2)}) copy-start(f32[2048]{0:T(1024)} %copy-done.35) | copy-start | bytes 24580
  760.5 11.3 %copy-start.46 = (f32[1024]{0:T(1024)S(1)}, f32[1024]{0:T(1024)}, u32[]{:S(2)}) copy-start(f32[1024]{0:T(1024)} %get-tuple-element.260) | copy-start | bytes 12292
  760.5 11.3 %copy-start.47 = (f32[1024]{0:T(1024)S(1)}, f32[1024]{0:T(1024)}, u32[]{:S(2)}) copy-start(f32[1024]{0:T(1024)} %get-tuple-element.256) | copy-start | bytes 12292
  760.5 11.3 %copy-start.48 = (f32[1024]{0:T(1024)S(1)}, f32[1024]{0:T(1024)}, u32[]{:S(2)}) copy-start(f32[1024]{0:T(1024)} %get-tuple-element.315) | copy-start | bytes 12292
  760.5 11.3 %copy-start.49 = (f32[1024]{0:T(1024)S(1)}, f32[1024]{0:T(1024)}, u32[]{:S(2)}) copy-start(f32[1024]{0:T(1024)} %get-tuple-element.321) | copy-start | bytes 12292
  760.6 11.3 %copy-start.52 = (f32[1024]{0:T(1024)S(1)}, f32[1024]{0:T(1024)}, u32[]{:S(2)}) copy-start(f32[1024]{0:T(1024)} %get-tuple-element.312) | copy-start | bytes 12292
  760.6 49.9 %copy-start.51 = (f32[1024]{0:T(1024)S(1)}, f32[1024]{0:T(1024)}, u32[]{:S(2)}) copy-start(f32[1024]{0:T(1024)} %param.29) | copy-start | bytes 12292
  810.4 281.8 %copy-start.1 = (bf16[1024,1024]{1,0:T(8,128)(2,1)S(1)}, bf16[1024,1024]{1,0:T(8,128)(2,1)}, u32[]{:S(2)}) copy-start(bf16[1024,1024]{1,0:T(8,128)(2,1)} %param.28) | copy-start | bytes 6291460
  (49 other events, 305.3 us)
Sparse Core Ops, SparseCore 0:
  105.4 88.1 all-reduce.4
  241.4 106.0 all-gather.2
  607.6 152.8 all-reduce.6
  764.0 75.9 reduce-scatter.4
  844.1 87.7 reduce-scatter.10
  936.0 87.9 reduce-scatter.8
  1027.9 64.2 reduce-scatter.6
